TPU v7x, 32 devices: a whole 2x2x4 slice. The times are simulated.
32 devices in a mesh: grp: 2 (over y), band: 4 (over x, core), ga: 4 (over z).
Axes of the slice: x: 2, y: 2, z: 4, core: 2. Of those that a mesh axis runs over, the one named last changes fastest.
Arguments:
- orbitals: bfloat16 [64, 8192], P(('grp', 'band'), 'ga'), parts along dimension 0, may hold values from -0.0625 to 0.0625
- energies: float32 [64], P(('grp', 'band')), parts along dimension 0, may hold values from -1.5 to -0.2
- projectors: bfloat16 [1024, 8192], P('grp', 'ga'), parts along dimension 0, may hold values from -0.125 to 0.125
- miller_index: int32 [3, 8192], P(None, 'ga'), may hold values from -12 to 12
- recip_scale: float32 [6], P('grp'), parts along dimension 0, may hold values from 0.06 to 0.14
- species: int32 [128], replicated, may hold values from 0 to 2
- proj_atom: int32 [512], replicated, may hold values from 0 to 127, as said below
- coupling: float32 [3, 4], replicated, may hold values from 0.5 to 3
Outputs:
- response: bfloat16 [3, 64, 8192], P(None, ('grp', 'band'), 'ga'), parts along dimension 1
- dielectric: float32 [6, 3], P('grp'), parts along dimension 0
- born: float32 [9, 256], P(None, 'grp'), parts along dimension 1
There are 2 independent parts, one for each index of `grp`. A program takes and returns all parts, laid end to end along the dimension named above; an argument that names none is the same for every part. Nothing has to cross between parts.
Inputs may be any that keep to these rules, and one draw needn't show every extreme that they name: `proj_atom`: every atom owns exactly 4 projectors.
All inputs are finite; a program needn't handle non-finite values.
Results may differ from a plain program's by a relative error of at most 0.015.
Values may be sent and summed in bfloat16 or wider, within the bound.
A program may use at most 64 MiB of HBM per device.

v0:
```python
import jax
import jax.numpy as jnp
from jax import lax
from jax.sharding import PartitionSpec as P

ITERS = 2
born_scale = 40.0


def tables(miller_index, recip_scale, species, proj_atom, coupling):
    natoms = species.shape[0]
    nspecies = coupling.shape[0]
    nchannels = coupling.shape[1]
    wavevec = miller_index.astype(jnp.float32) * recip_scale[:, None]
    kinetic = 0.5 * jnp.sum(wavevec * wavevec, axis=0)
    atom_onehot = (proj_atom[:, None] == jnp.arange(natoms, dtype=jnp.int32)[None, :]).astype(
        jnp.float32
    )
    spec_proj = jnp.dot(atom_onehot, species.astype(jnp.float32), precision=lax.Precision.HIGHEST)
    spec_onehot = (spec_proj[:, None] == jnp.arange(nspecies, dtype=jnp.float32)[None, :]).astype(
        jnp.float32
    )
    channel = jnp.arange(proj_atom.shape[0], dtype=jnp.int32) % nchannels
    chan_onehot = (channel[:, None] == jnp.arange(nchannels, dtype=jnp.int32)[None, :]).astype(
        jnp.float32
    )
    strength = jnp.sum(
        jnp.dot(spec_onehot, coupling, precision=lax.Precision.HIGHEST) * chan_onehot, axis=1
    )
    return (wavevec, kinetic, atom_onehot, strength)


def per_device(
    orbitals, energies, projectors, miller_index, recip_scale, species, proj_atom, coupling
):
    bands = orbitals.shape[0]
    width = orbitals.shape[1]
    nproj = projectors.shape[0]
    total_bands = bands * lax.axis_size("band")
    wavevec, kinetic, atom_onehot, strength = tables(
        miller_index, recip_scale, species, proj_atom, coupling
    )
    precond = 1.0 / (1.0 + kinetic)

    def conduct(values):
        flat = values.reshape(3 * bands, width)
        block = jnp.dot(
            lax.all_gather(orbitals, "band", axis=0, tiled=True),
            flat.T,
            preferred_element_type=jnp.float32,
        )
        margin = lax.psum(block, "ga").astype(jnp.bfloat16)
        removed = jnp.dot(
            margin.T,
            lax.all_gather(orbitals, "band", axis=0, tiled=True),
            preferred_element_type=jnp.float32,
        )
        return (flat.astype(jnp.float32) - removed).reshape(3, bands, width)

    orb_float = orbitals.astype(jnp.float32)
    stacked = jnp.concatenate([orb_float[None], wavevec[:, None, :] * orb_float[None]], 0).astype(
        jnp.bfloat16
    )
    proj_local = jnp.dot(
        stacked.reshape(4 * bands, width), projectors.T, preferred_element_type=jnp.float32
    )
    proj = lax.psum(proj_local, "ga").reshape(4, bands, nproj)
    weighted = (strength * proj).astype(jnp.bfloat16)
    returned = jnp.dot(
        weighted.reshape(4 * bands, nproj), projectors, preferred_element_type=jnp.float32
    ).reshape(4, bands, width)
    commutator = (wavevec[:, None, :] * (orb_float + returned[0])[None] + returned[1:]).astype(
        jnp.bfloat16
    )
    source = -conduct(commutator)
    response = jnp.zeros_like(source)
    residual = source
    resp_proj = jnp.zeros((3, bands, nproj), jnp.float32)
    diag_shift = kinetic[None, None, :] - energies[None, :, None]
    for step in range(ITERS):
        search = conduct((precond * residual).astype(jnp.bfloat16))
        search_low = search.astype(jnp.bfloat16)
        dir_local = jnp.dot(
            search_low.reshape(3 * bands, width), projectors.T, preferred_element_type=jnp.float32
        )
        num_local = jnp.sum(residual * search, axis=2)
        diag_local = jnp.sum(diag_shift * search * search, axis=2)
        dir_proj, numerator, diag_part = lax.psum((dir_local, num_local, diag_local), "ga")
        dir_proj = dir_proj.reshape(3, bands, nproj)
        dir_weight = (strength * dir_proj).astype(jnp.bfloat16)
        image = diag_shift * search + jnp.dot(
            dir_weight.reshape(3 * bands, nproj), projectors, preferred_element_type=jnp.float32
        ).reshape(3, bands, width)
        curvature = diag_part + jnp.sum(dir_weight.astype(jnp.float32) * dir_proj, axis=2)
        step_size = numerator / curvature
        response = response + step_size[:, :, None] * search
        residual = residual - step_size[:, :, None] * image
        resp_proj = resp_proj + step_size[:, :, None] * dir_proj
    diel_local = jnp.einsum("anx,bnx->ab", response, source, precision=lax.Precision.HIGHEST)
    dielectric = jnp.eye(3, dtype=jnp.float32) + 4.0 / total_bands * lax.psum(
        diel_local, ("band", "ga")
    )
    pair = jnp.einsum("anp,bnp->abp", resp_proj, proj[1:], precision=lax.Precision.HIGHEST)
    born_local = jnp.dot(
        (pair * strength).reshape(9, nproj), atom_onehot, precision=lax.Precision.HIGHEST
    )
    born = born_scale * lax.psum(born_local, "band")
    return (response.astype(jnp.bfloat16), dielectric, born)


def solution(mesh):
    placed = (
        P(("grp", "band"), "ga"),
        P(("grp", "band")),
        P("grp", "ga"),
        P(None, "ga"),
        P("grp"),
        P(),
        P(),
        P(),
    )
    return jax.shard_map(
        per_device,
        mesh=mesh,
        in_specs=placed,
        out_specs=(P(None, ("grp", "band"), "ga"), P("grp", None), P(None, "grp")),
        check_vma=False,
    )
```

profile of v0, /device:TPU:0, one launch (start us, length us, event | category | flops | bytes accessed | tf_op | source)
XLA Modules:
  0.0 192.2 jit_solution(5939086287881664296)
XLA Ops:
  7.3 0.9 convert_element_type.82
  8.2 0.9 multiply_reduce_fusion.3
  9.1 2.1 %fusion.18 = f32[32,512]{1,0:T(8,128)} fusion(bf16[512,2048]{1,0:T(8,128)(2,1)S(1)} %copy-done, bf16[3,8,2048]{2,1,0:T(8,128)(2,1)S(1)} %multiply_convert_fusion.2, bf16[1,8,2048]{2,1,0:T(8,128)(2,1)} %bitcast.93), kind=kOutput, calls=%fused_computation.43 | convolution fusion | flops 67174400 | bytes 2293760 | tf_op jit(solution)/shard_map/dot_general | solution.py:64
  12.0 6.5 %all_gather.2 = bf16[32,2048]{1,0:T(8,128)(2,1)S(1)} all-gather(bf16[8,2048]{1,0:T(8,128)(2,1)S(1)} %copy-done.1), channel_id=1, replica_groups=mesh['grp'=2,'band'=4,'ga'=4] {'band'}, dimensions={0}, use_global_device_ids=true | all-gather | bytes 163840 | tf_op jit(solution)/shard_map/all_gather | solution.py:48
  18.5 29.9 %all-reduce.4.cloned.1.call-done = f32[32,512]{1,0:T(8,128)} async-done(((f32[32,512]{1,0:T(8,128)}), f32[32,512]{1,0:T(8,128)}) %all-reduce.4.cloned.1.call-update) | async-done | bytes 65552 | tf_op jit(solution)/shard_map/psum | solution.py:67
  48.4 1.3 fusion.32
  49.9 17.5 %psum.85 = bf16[32,24]{0,1:T(8,128)(2,1)S(1)} all-reduce(f32[32,24]{0,1:T(8,128)S(1)} %convolution_bitcast_fusion.2), channel_id=1, replica_groups=mesh['grp'=2,'band'=4,'ga'=4] {'ga'}, use_global_device_ids=true, to_apply=%region_2.3 | all-reduce | flops 768 | bytes 4608 | tf_op jit(solution)/shard_map/psum | solution.py:52
  67.7 15.6 %psum.86 = bf16[32,24]{0,1:T(8,128)(2,1)S(1)} all-reduce(f32[32,24]{0,1:T(8,128)S(1)} %convolution_bitcast_fusion.1), channel_id=1, replica_groups=mesh['grp'=2,'band'=4,'ga'=4] {'ga'}, use_global_device_ids=true, to_apply=%region_4.5 | all-reduce | flops 768 | bytes 4608 | tf_op jit(solution)/shard_map/psum | solution.py:52
  83.8 0.7 fusion.27
  84.5 17.3 %all-reduce.1 = (f32[3,8]{1,0:T(4,128)S(1)}, f32[3,8]{1,0:T(4,128)S(1)}, f32[24,512]{1,0:T(8,128)S(1)}) all-reduce(f32[3,8]{1,0:T(4,128)S(1)} %reduce_sum.85, f32[3,8]{1,0:T(4,128)S(1)} %reduce_sum.87, f32[24,512]{1,0:T(8,128)S(1)} %fusion.27), channel_id=1, replica_groups=mesh['grp'=2,'band'=4,'ga'=4] {'ga'}, use_global_device_ids=true, to_apply=%region_6.7 | all-reduce | flops 12336 | bytes 98688 | tf_op jit(solution)/shard_map/psum | solution.py:88
  102.0 0.4 fusion.2
  102.6 16.5 %psum.90 = bf16[32,24]{0,1:T(8,128)(2,1)S(1)} all-reduce(f32[32,24]{0,1:T(8,128)S(1)} %convolution_bitcast_fusion), channel_id=1, replica_groups=mesh['grp'=2,'band'=4,'ga'=4] {'ga'}, use_global_device_ids=true, to_apply=%region_11.12 | all-reduce | flops 768 | bytes 4608 | tf_op jit(solution)/shard_map/psum | solution.py:52
  119.5 0.7 fusion.25
  120.2 16.3 %all-reduce = (f32[3,8]{1,0:T(4,128)S(1)}, f32[3,8]{1,0:T(4,128)S(1)}, f32[24,512]{1,0:T(8,128)S(1)}) all-reduce(f32[3,8]{1,0:T(4,128)S(1)} %get-tuple-element.16, f32[3,8]{1,0:T(4,128)S(1)} %reduce_sum.92, f32[24,512]{1,0:T(8,128)S(1)} %fusion.25), channel_id=1, replica_groups=mesh['grp'=2,'band'=4,'ga'=4] {'ga'}, use_global_device_ids=true, to_apply=%region_13.14 | all-reduce | flops 12336 | bytes 98688 | tf_op jit(solution)/shard_map/psum | solution.py:88
  136.8 0.7 fusion.17
  137.7 1.4 convolution_bitcast_fusion.3
  139.1 29.7 %psum.94 = f32[3,3]{1,0:T(4,128)S(1)} all-reduce(f32[3,3]{1,0:T(4,128)S(1)} %convolution_bitcast_fusion.3), channel_id=1, replica_groups=mesh['grp'=2,'band'=4,'ga'=4] {'band','ga'}, use_global_device_ids=true, to_apply=%region_18.19 | all-reduce | flops 9 | bytes 72 | tf_op jit(solution)/shard_map/psum | solution.py:100
  168.9 0.6 multiply_add_fusion
  169.5 0.4 copy.25
  169.9 1.3 copy.24
  171.2 5.9 %fusion.4 = f32[3,3,512]{0,1,2:T(4,128)} fusion(f32[3,8,512]{1,0,2:T(4,128)} %copy.24, f32[3,8,512]{1,0,2:T(4,128)S(1)} %copy.25, f32[512]{0:T(512)S(1)} %fusion.5), kind=kOutput, calls=%fused_computation.9 | convolution fusion | flops 446976 | bytes 118784 | tf_op jit(solution)/shard_map/anp,bnp->abp/dot_general | solution.py:103
  177.1 1.6 copy.26
  179.0 5.8 %psum.95 = f32[9,128]{1,0:T(8,128)S(1)} all-reduce(f32[9,128]{1,0:T(8,128)S(1)} %fusion.10), channel_id=1, replica_groups=mesh['grp'=2,'band'=4,'ga'=4] {'band'}, use_global_device_ids=true, to_apply=%region_19.20 | all-reduce | flops 1152 | bytes 9216 | tf_op jit(solution)/shard_map/psum | solution.py:107
  184.8 0.6 broadcast_multiply_fusion
  (46 shorter events, 3.5 us)
Async XLA Ops:
  7.2 1.9 copy-start
  7.2 4.8 %copy-start.1 = (bf16[8,2048]{1,0:T(8,128)(2,1)S(1)}, bf16[8,2048]{1,0:T(8,128)(2,1)}, u32[]{:S(2)}) copy-start(bf16[8,2048]{1,0:T(8,128)(2,1)} %param.8) | copy-start | bytes 98308
  7.2 4.1 %copy-start.5 = (s32[512]{0:T(512)S(1)}, s32[512]{0:T(512)}, u32[]{:S(2)}) copy-start(s32[512]{0:T(512)} %param.14) | copy-start | bytes 6148
  7.2 4.1 %copy-start.6 = (s32[128]{0:T(128)S(1)}, s32[128]{0:T(128)}, u32[]{:S(2)}) copy-start(s32[128]{0:T(128)} %param.13) | copy-start | bytes 1540
  7.2 4.4 %copy-start.3 = (f32[8]{0:T(128)S(1)}, f32[8]{0:T(128)}, u32[]{:S(2)}) copy-start(f32[8]{0:T(128)} %param.9) | copy-start | bytes 100
  7.2 4.4 %copy-start.4 = (f32[3,4]{1,0:T(4,128)S(1)}, f32[3,4]{1,0:T(4,128)}, u32[]{:S(2)}) copy-start(f32[3,4]{1,0:T(4,128)} %param.15) | copy-start | bytes 148
  7.2 41.2 %all-reduce.4.cloned.1.call-start = ((), (), s32[]{:S(2)}) async-start(), calls=%async_computation | async-start | bytes 131072 | tf_op jit(solution)/shard_map/psum | solution.py:67
  119.5 50.4 %copy-start.2 = (f32[32,512]{1,0:T(8,128)S(1)}, f32[32,512]{1,0:T(8,128)}, u32[]{:S(2)}) copy-start(f32[32,512]{1,0:T(8,128)} %all-reduce.4.cloned.1.call-done) | copy-start | bytes 196612
Sparse Core Ops, SparseCore 0:
  11.3 37.0 all-reduce.3
where the time goes:
time: 193 us; the launch traced here: 192 us
  blocking collectives  125 us (65%)
  waiting for transfers between devices  29.9 us (15%)
  matrix products  14.5 us (8%)
  between operations  14.2 us (7%)
  other arithmetic  4.39 us (2%)
  local copies, waits for them, and re-layouts  3.93 us (2%)
    psum x3, blocking collectives, conduct(): margin = lax.psum(block, 'ga').astype(jnp.bfloat16)  49.6 us
    psum x2, blocking collectives, per_device(): lax.psum((dir_local, num_local, diag_local), 'ga')  33.6 us
    psum x1, waiting for transfers between devices, per_device(): proj = lax.psum(proj_local, 'ga').reshape(4, bands, nproj)  29.9 us
    psum x1, blocking collectives, per_device(): lax.psum(diel_local, ('band', 'ga'))  29.7 us
    all_gather x1, blocking collectives, conduct(): lax.all_gather(orbitals, 'band', axis=0, tiled=True)  6.51 us
    dot_general x1, matrix products, per_device(): jnp.einsum('anp,bnp->abp', resp_proj, proj[1:], precision=lax.Precision.H...  5.93 us
    psum x1, blocking collectives, per_device(): born = born_scale * lax.psum(born_local, 'band')  5.77 us
  transfers between devices with their start and end apart: 1, of which 1 were waited for; matrix products, arithmetic and copies ran while one was open for 0% of the time, Pallas kernels for 0%

commit v1 on v0

--- a/solution.py
+++ b/solution.py
@@ -49,7 +49,7 @@
             flat.T,
             preferred_element_type=jnp.float32,
         )
-        margin = lax.psum(block, "ga").astype(jnp.bfloat16)
+        margin = jnp.sum(lax.all_gather(block, "ga"), axis=0).astype(jnp.bfloat16)
         removed = jnp.dot(
             margin.T,
             lax.all_gather(orbitals, "band", axis=0, tiled=True),

time: 193 us -> 184 us (0.953)
  blocking collectives: 125 us -> 116 us
    psum x3 -> x0, blocking collectives: 49.6 us -> none  [conduct(): margin = lax.psum(block, 'ga').astype(jnp.bfloat16)]
    all_gather x0 -> x3, blocking collectives: none -> 39.2 us  [conduct(): margin = jnp.sum(lax.all_gather(block, 'ga'), axis=0).astype(jnp.bfloat16)]
where the time goes in v1:
time: 184 us; the launch traced here: 183 us
  blocking collectives  116 us (63%)
  waiting for transfers between devices  29.9 us (16%)
  matrix products  14.5 us (8%)
  between operations  14.3 us (8%)
  other arithmetic  4.42 us (2%)
  local copies, waits for them, and re-layouts  3.93 us (2%)
    all_gather x3, blocking collectives, conduct(): margin = jnp.sum(lax.all_gather(block, 'ga'), axis=0).astype(jnp.bfloat16)  39.2 us
    psum x2, blocking collectives, per_device(): lax.psum((dir_local, num_local, diag_local), 'ga')  34.9 us
    psum x1, waiting for transfers between devices, per_device(): proj = lax.psum(proj_local, 'ga').reshape(4, bands, nproj)  29.9 us
    psum x1, blocking collectives, per_device(): lax.psum(diel_local, ('band', 'ga'))  29.7 us
    all_gather x1, blocking collectives, conduct(): lax.all_gather(orbitals, 'band', axis=0, tiled=True)  6.51 us
    dot_general x1, matrix products, per_device(): jnp.einsum('anp,bnp->abp', resp_proj, proj[1:], precision=lax.Precision.H...  5.93 us
    psum x1, blocking collectives, per_device(): born = born_scale * lax.psum(born_local, 'band')  5.77 us
  transfers between devices with their start and end apart: 1, of which 1 were waited for; matrix products, arithmetic and copies ran while one was open for 0% of the time, Pallas kernels for 0%

profile of v1, /device:TPU:0, one launch (start us, length us, event | category | flops | bytes accessed | tf_op | source)
XLA Modules:
  0.0 183.1 jit_solution(13177537103049888617)
XLA Ops:
  7.3 0.9 convert_element_type.82
  8.2 0.9 multiply_reduce_fusion.3
  9.1 2.1 %fusion.18 = f32[32,512]{1,0:T(8,128)} fusion(bf16[512,2048]{1,0:T(8,128)(2,1)S(1)} %copy-done, bf16[3,8,2048]{2,1,0:T(8,128)(2,1)S(1)} %multiply_convert_fusion.2, bf16[1,8,2048]{2,1,0:T(8,128)(2,1)} %bitcast.99), kind=kOutput, calls=%fused_computation.43 | convolution fusion | flops 67174400 | bytes 2293760 | tf_op jit(solution)/shard_map/dot_general | solution.py:64
  12.0 6.5 %all_gather.26 = bf16[32,2048]{1,0:T(8,128)(2,1)S(1)} all-gather(bf16[8,2048]{1,0:T(8,128)(2,1)S(1)} %copy-done.1), channel_id=1, replica_groups=mesh['grp'=2,'band'=4,'ga'=4] {'band'}, dimensions={0}, use_global_device_ids=true | all-gather | bytes 163840 | tf_op jit(solution)/shard_map/all_gather | solution.py:48
  18.5 29.9 %all-reduce.4.cloned.1.call-done = f32[32,512]{1,0:T(8,128)} async-done(((f32[32,512]{1,0:T(8,128)}), f32[32,512]{1,0:T(8,128)}) %all-reduce.4.cloned.1.call-update) | async-done | bytes 65552 | tf_op jit(solution)/shard_map/psum | solution.py:67
  48.4 1.3 fusion.32
  49.9 13.1 %all-gather.3 = f32[4,32,24]{1,2,0:T(8,128)S(1)} all-gather(f32[1,32,24]{1,2,0:T(8,128)S(1)} %convolution_bitcast_fusion.2), channel_id=2, replica_groups=mesh['grp'=2,'band'=4,'ga'=4] {'ga'}, dimensions={0}, use_global_device_ids=true | all-gather | bytes 15360 | tf_op jit(solution)/shard_map/all_gather | solution.py:52
  63.3 13.1 %all-gather.4 = f32[4,32,24]{1,2,0:T(8,128)S(1)} all-gather(f32[1,32,24]{1,2,0:T(8,128)S(1)} %convolution_bitcast_fusion.1), channel_id=3, replica_groups=mesh['grp'=2,'band'=4,'ga'=4] {'ga'}, dimensions={0}, use_global_device_ids=true | all-gather | bytes 15360 | tf_op jit(solution)/shard_map/all_gather | solution.py:52
  76.9 0.7 fusion.27
  77.5 18.4 %all-reduce.1 = (f32[3,8]{1,0:T(4,128)S(1)}, f32[3,8]{1,0:T(4,128)S(1)}, f32[24,512]{1,0:T(8,128)S(1)}) all-reduce(f32[3,8]{1,0:T(4,128)S(1)} %reduce_sum.114, f32[3,8]{1,0:T(4,128)S(1)} %reduce_sum.116, f32[24,512]{1,0:T(8,128)S(1)} %fusion.27), channel_id=1, replica_groups=mesh['grp'=2,'band'=4,'ga'=4] {'ga'}, use_global_device_ids=true, to_apply=%region_6.7 | all-reduce | flops 12336 | bytes 98688 | tf_op jit(solution)/shard_map/psum | solution.py:88
  96.3 0.4 fusion.2
  96.8 13.1 %all-gather.5 = f32[4,32,24]{1,2,0:T(8,128)S(1)} all-gather(f32[1,32,24]{1,2,0:T(8,128)S(1)} %convolution_bitcast_fusion), channel_id=4, replica_groups=mesh['grp'=2,'band'=4,'ga'=4] {'ga'}, dimensions={0}, use_global_device_ids=true | all-gather | bytes 15360 | tf_op jit(solution)/shard_map/all_gather | solution.py:52
  110.3 0.7 fusion.25
  111.1 16.4 %all-reduce = (f32[3,8]{1,0:T(4,128)S(1)}, f32[3,8]{1,0:T(4,128)S(1)}, f32[24,512]{1,0:T(8,128)S(1)}) all-reduce(f32[3,8]{1,0:T(4,128)S(1)} %get-tuple-element.16, f32[3,8]{1,0:T(4,128)S(1)} %reduce_sum.122, f32[24,512]{1,0:T(8,128)S(1)} %fusion.25), channel_id=1, replica_groups=mesh['grp'=2,'band'=4,'ga'=4] {'ga'}, use_global_device_ids=true, to_apply=%region_13.14 | all-reduce | flops 12336 | bytes 98688 | tf_op jit(solution)/shard_map/psum | solution.py:88
  127.8 0.7 fusion.17
  128.6 1.4 convolution_bitcast_fusion.3
  130.1 29.7 %psum.70 = f32[3,3]{1,0:T(4,128)S(1)} all-reduce(f32[3,3]{1,0:T(4,128)S(1)} %convolution_bitcast_fusion.3), channel_id=1, replica_groups=mesh['grp'=2,'band'=4,'ga'=4] {'band','ga'}, use_global_device_ids=true, to_apply=%region_18.19 | all-reduce | flops 9 | bytes 72 | tf_op jit(solution)/shard_map/psum | solution.py:100
  159.8 0.6 multiply_add_fusion
  160.4 0.4 copy.31
  160.8 1.3 copy.30
  162.1 5.9 %fusion.4 = f32[3,3,512]{0,1,2:T(4,128)} fusion(f32[3,8,512]{1,0,2:T(4,128)} %copy.30, f32[3,8,512]{1,0,2:T(4,128)S(1)} %copy.31, f32[512]{0:T(512)S(1)} %fusion.5), kind=kOutput, calls=%fused_computation.9 | convolution fusion | flops 446976 | bytes 118784 | tf_op jit(solution)/shard_map/anp,bnp->abp/dot_general | solution.py:103
  168.0 1.6 copy.32
  169.9 5.8 %psum.71 = f32[9,128]{1,0:T(8,128)S(1)} all-reduce(f32[9,128]{1,0:T(8,128)S(1)} %fusion.10), channel_id=1, replica_groups=mesh['grp'=2,'band'=4,'ga'=4] {'band'}, use_global_device_ids=true, to_apply=%region_19.20 | all-reduce | flops 1152 | bytes 9216 | tf_op jit(solution)/shard_map/psum | solution.py:107
  175.7 0.6 broadcast_multiply_fusion
  (49 shorter events, 3.6 us)
Async XLA Ops:
  7.2 1.9 %copy-start = (bf16[512,2048]{1,0:T(8,128)(2,1)S(1)}, bf16[512,2048]{1,0:T(8,128)(2,1)}, u32[]{:S(2)}) copy-start(bf16[512,2048]{1,0:T(8,128)(2,1)} %param.10) | copy-start | bytes 6291460
  7.2 4.8 %copy-start.1 = (bf16[8,2048]{1,0:T(8,128)(2,1)S(1)}, bf16[8,2048]{1,0:T(8,128)(2,1)}, u32[]{:S(2)}) copy-start(bf16[8,2048]{1,0:T(8,128)(2,1)} %param.8) | copy-start | bytes 98308
  7.2 4.1 %copy-start.5 = (s32[512]{0:T(512)S(1)}, s32[512]{0:T(512)}, u32[]{:S(2)}) copy-start(s32[512]{0:T(512)} %param.14) | copy-start | bytes 6148
  7.2 4.1 %copy-start.6 = (s32[128]{0:T(128)S(1)}, s32[128]{0:T(128)}, u32[]{:S(2)}) copy-start(s32[128]{0:T(128)} %param.13) | copy-start | bytes 1540
  7.2 4.4 %copy-start.3 = (f32[8]{0:T(128)S(1)}, f32[8]{0:T(128)}, u32[]{:S(2)}) copy-start(f32[8]{0:T(128)} %param.9) | copy-start | bytes 100
  7.2 4.4 %copy-start.4 = (f32[3,4]{1,0:T(4,128)S(1)}, f32[3,4]{1,0:T(4,128)}, u32[]{:S(2)}) copy-start(f32[3,4]{1,0:T(4,128)} %param.15) | copy-start | bytes 148
  7.2 41.2 %all-reduce.4.cloned.1.call-start = ((), (), s32[]{:S(2)}) async-start(), calls=%async_computation | async-start | bytes 131072 | tf_op jit(solution)/shard_map/psum | solution.py:67
  110.3 50.4 %copy-start.2 = (f32[32,512]{1,0:T(8,128)S(1)}, f32[32,512]{1,0:T(8,128)}, u32[]{:S(2)}) copy-start(f32[32,512]{1,0:T(8,128)} %all-reduce.4.cloned.1.call-done) | copy-start | bytes 196612
Sparse Core Ops, SparseCore 0:
  11.3 37.0 all-reduce.3
